TPU v7x, 32 devices: a whole 2x2x4 slice. The times are simulated.
32 devices in a mesh: dp: 8 (over z, x), mp: 4 (over y, core).
Axes of the slice: x: 2, y: 2, z: 4, core: 2. Of those that a mesh axis runs over, the one named last changes fastest.
Arguments:
- features: bfloat16 [2048, 512], P('dp'), may hold values from -6 to 6
- adjacency: bfloat16 [64, 32, 128, 128], P('dp'), may hold values from -0.125 to 0.125
- source_block: int32 [64, 32], P('dp'), may hold values from 0 to 1
- edge_type: int32 [64, 32], P('dp'), may hold values from 0 to 19
- target_block: int32 [64, 32], P('dp'), may hold values from 0 to 1
- live_count: int32 [8, 8], P('dp'), may hold values from 24 to 32, as said below
- relation_weight: bfloat16 [20, 512, 512], P(None, None, 'mp'), may hold values from -0.25 to 0.25
- self_weight: bfloat16 [512, 512], P(None, 'mp'), may hold values from -0.25 to 0.25
- layer_bias: bfloat16 [512], P('mp'), may hold values from -3 to 3
- norm_gain: bfloat16 [512], replicated, may hold values from 0.5 to 1.5
Outputs:
- node_states: bfloat16 [2048, 512], P(('dp', 'mp'))
Inputs may be any that keep to these rules, and one draw needn't show every extreme that they name: `source_block`: row s * 8 + d names a block among sender s's 2 blocks. `target_block`: row d * 8 + s names a block among receiver d's 2 blocks. live_count[d, s] live slots from sender s to receiver d, the first ones; some receiver has all 32 slots live from every sender.
All inputs are finite; a program needn't handle non-finite values.
Results may differ from a plain program's by a relative error of at most 0.007.
Values may be sent and summed in bfloat16 or wider, within the bound.
A program may use at most 128 MiB of HBM per device.

v0:
```python
import jax
import jax.numpy as jnp
from jax import lax
from jax.sharding import PartitionSpec as P

BLK = 128


epsilon = 1e-05


def block_table(features, relation_weight, blocks):
    stacked = features.reshape(blocks, BLK, features.shape[1])
    lookup = jnp.einsum(
        "bid,rdc->bric", stacked, relation_weight, preferred_element_type=jnp.float32
    )
    return lookup.astype(jnp.bfloat16).reshape(
        blocks * relation_weight.shape[0], BLK, relation_weight.shape[2]
    )


def transform_slots(lookup, lookup_rows, adj_tiles):
    chosen = jnp.take(lookup, lookup_rows, axis=0)
    return jnp.einsum("nij,njc->nic", adj_tiles, chosen, preferred_element_type=jnp.float32)


def selector(targets, counts, blocks):
    slot_count = targets.shape[1]
    active = jnp.arange(slot_count, dtype=jnp.int32)[None, :] < counts[:, None]
    matches = targets[:, :, None] == jnp.arange(blocks, dtype=jnp.int32)[None, None, :]
    return jnp.logical_and(matches, active[:, :, None]).astype(jnp.float32)


def per_device(
    features,
    adjacency,
    source_block,
    edge_type,
    target_block,
    live_count,
    relation_weight,
    self_weight,
    layer_bias,
    norm_gain,
):
    peer_count = lax.axis_size("dp")
    slot_count = source_block.shape[1]
    node_rows = features.shape[0]
    blocks = node_rows // BLK
    columns = relation_weight.shape[2]
    lookup = block_table(features, relation_weight, blocks)
    lookup_rows = (source_block * relation_weight.shape[0] + edge_type).reshape(
        peer_count * slot_count
    )
    flat_tiles = adjacency.reshape(peer_count * slot_count, BLK, BLK)
    routed, routed_count = (
        lax.all_to_all(target_block, "dp", split_axis=0, concat_axis=0, tiled=True),
        lax.all_to_all(
            live_count.reshape(peer_count, 1), "dp", split_axis=0, concat_axis=0, tiled=True
        ),
    )
    weights = selector(routed, routed_count[:, 0], blocks)
    receivers = node_rows * lax.axis_size("dp") // node_rows
    message = transform_slots(lookup, lookup_rows, flat_tiles).reshape(
        receivers, slot_count, BLK * columns
    )
    summed = jnp.einsum("rkb,rkx->rbx", weights, message, precision=lax.Precision.HIGHEST)
    aggregate = lax.psum_scatter(
        summed.reshape(receivers * blocks * BLK, columns), "dp", scatter_dimension=0, tiled=True
    )
    own_term = jnp.dot(features, self_weight, preferred_element_type=jnp.float32)
    hidden = jax.nn.relu(own_term + aggregate + layer_bias.astype(jnp.float32)).astype(jnp.bfloat16)
    by_rows = lax.all_to_all(hidden, "mp", split_axis=0, concat_axis=1, tiled=True)
    values = by_rows.astype(jnp.float32)
    inverse_rms = lax.rsqrt(jnp.mean(values * values, axis=1, keepdims=True) + epsilon)
    return (values * inverse_rms * norm_gain.astype(jnp.float32)).astype(jnp.bfloat16)


def solution(mesh):
    return jax.shard_map(
        per_device,
        mesh=mesh,
        in_specs=(
            P("dp", None),
            P("dp", None, None, None),
            P("dp", None),
            P("dp", None),
            P("dp", None),
            P("dp", None),
            P(None, None, "mp"),
            P(None, "mp"),
            P("mp"),
            P(),
        ),
        out_specs=P(("dp", "mp"), None),
        check_vma=False,
    )
```

profile of v0, /device:TPU:0, one launch (start us, length us, event | category | flops | bytes accessed | tf_op | source)
XLA Modules:
  0.0 182.4 jit_solution(16302394386973971121)
XLA Ops:
  6.5 0.0 copy-start
  6.5 1.5 copy.24
  8.0 7.3 %all-to-all-start.1 = ((s32[8,1,1]{2,1,0:T(1,128)}), s32[8,1,1]{2,1,0:T(1,128)S(1)}, u32[]{:S(2)}, u32[]{:S(2)}) async-start(s32[8,1,1]{2,1,0:T(1,128)} %copy.24), calls=%async_computation.1 | async-start | bytes 8192 | tf_op jit(solution)/shard_map/all_to_all | solution.py:58
  15.3 0.7 multiply_add_fusion
  16.0 0.1 reshape.104
  16.1 0.1 reshape.101
  16.2 0.0 copy-done
  16.2 2.9 %fusion.8 = bf16[2,20,128,128]{2,3,0,1:T(8,128)(2,1)} fusion(bf16[2,128,512,1]{2,1,0,3:T(8,128)(2,1)} %bitcast.40, bf16[20,512,128]{2,1,0:T(8,128)(2,1)S(1)} %copy-done), kind=kOutput, calls=%fused_computation.8 | convolution fusion | flops 671744000 | bytes 4194304 | tf_op jit(solution)/shard_map/bid,rdc->bric/dot_general | solution.py:14
  19.1 1.8 copy.26
  20.9 8.6 %gather_fusion = bf16[256,128,128]{2,1,0:T(8,128)(2,1)} fusion(bf16[40,128,128]{2,1,0:T(8,128)(2,1)S(1)} %bitcast.38, s32[1024]{0:T(1024)S(1)} %pad_clamp_fusion), kind=kCustom, calls=%fused_computation | custom fusion | bytes 16778240 | tf_op jit(solution)/shard_map/jit(_take)/gather | solution.py:23
  29.5 13.2 %convolution_bitcast_fusion = f32[256,128,128]{1,2,0:T(8,128)} fusion(bf16[256,128,128]{2,1,0:T(8,128)(2,1)} %bitcast.39, bf16[256,128,128]{2,1,0:T(8,128)(2,1)} %gather_fusion, pred[256]{0:T(512)(128)(4,1)S(1)} %compare_and_fusion), kind=kOutput, calls=%fused_computation.1 | convolution fusion | flops 1077936128 | bytes 33554688 | tf_op jit(solution)/shard_map/nij,njc->nic/dot_general | solution.py:24
  42.7 17.4 %copy.28 = f32[256,128,128]{2,1,0:T(8,128)} copy(f32[256,128,128]{1,2,0:T(8,128)} %convolution_bitcast_fusion) | data formatting | bytes 33554432 | tf_op jit(solution)/shard_map/nij,njc->nic/dot_general | solution.py:24
  60.2 18.2 %reshape.106 = f32[8,32,16384]{2,1,0:T(8,128)} reshape(f32[256,128,128]{2,1,0:T(8,128)} %copy.28) | data formatting | bytes 33554432 | tf_op jit(solution)/shard_map/reshape | solution.py:64
  78.4 0.0 all-to-all-done.1
  78.4 6.0 %all-to-all-start = ((s32[8,1,32]{2,1,0:T(1,128)}), s32[8,1,32]{2,1,0:T(1,128)S(1)}, u32[]{:S(2)}, u32[]{:S(2)}) async-start(s32[8,1,32]{2,1,0:T(1,128)} %bitcast), calls=%async_computation | async-start | bytes 8192 | tf_op jit(solution)/shard_map/all_to_all | solution.py:57
  84.4 0.0 reduce-scatter.2.cloned.1.call-start
  84.4 0.2 reduce.2
  84.7 0.1 iota_compare_fusion
  84.7 6.1 %all-to-all-done = s32[8,1,32]{2,1,0:T(1,128)S(1)} async-done(((s32[8,1,32]{2,1,0:T(1,128)}), s32[8,1,32]{2,1,0:T(1,128)S(1)}, u32[]{:S(2)}, u32[]{:S(2)}) %all-to-all-start) | async-done | bytes 1056 | tf_op jit(solution)/shard_map/all_to_all | solution.py:57
  90.8 0.0 copy-start.1
  90.8 0.0 copy-start.5
  90.8 0.0 copy-start.2
  90.8 0.0 copy-start.3
  90.8 0.0 copy-start.4
  90.8 10.0 %fusion.17 = f32[8,2,16384]{2,1,0:T(2,128)} fusion(f32[8,32,16384]{2,1,0:T(8,128)} %reshape.106, pred[8,32]{1,0:T(8,128)(4,1)S(1)} %iota_compare_fusion, s32[8,32]{1,0:T(8,128)S(1)} %bitcast.41), kind=kOutput, calls=%fused_computation.19 | convolution fusion | flops 100664320 | bytes 17827072 | tf_op jit(solution)/shard_map/rkb,rkx->rbx/dot_general | solution.py:67
  100.8 3.1 %reshape.107 = f32[2048,128]{1,0:T(8,128)} reshape(f32[8,2,16384]{2,1,0:T(2,128)} %fusion.17) | data formatting | bytes 2097152 | tf_op jit(solution)/shard_map/reshape | solution.py:69
  103.9 0.0 reduce-scatter.2.cloned.1.call-update
  104.0 0.0 copy-done.5
  104.0 61.6 %reduce-scatter.2.cloned.1.call-done = f32[256,128]{1,0:T(8,128)} async-done(((f32[2048,128]{1,0:T(8,128)}), f32[256,128]{1,0:T(8,128)}) %reduce-scatter.2.cloned.1.call-update) | async-done | bytes 131088 | tf_op jit(solution)/shard_map/reduce_scatter | solution.py:68
  165.6 0.0 copy-done.2
  165.6 0.0 copy-done.3
  165.6 1.7 fusion.13
  167.3 3.3 %all-to-all-start.2 = ((bf16[4,64,128]{2,1,0:T(8,128)(2,1)}), bf16[4,64,128]{2,1,0:T(8,128)(2,1)S(1)}, u32[]{:S(2)}, u32[]{:S(2)}) async-start(bf16[4,64,128]{2,1,0:T(8,128)(2,1)} %bitcast.11), calls=%async_computation.3 | async-start | bytes 131072 | tf_op jit(solution)/shard_map/all_to_all | solution.py:73
  170.6 0.0 copy-done.4
  170.7 4.1 %all-to-all-done.2 = bf16[4,64,128]{2,1,0:T(8,128)(2,1)S(1)} async-done(((bf16[4,64,128]{2,1,0:T(8,128)(2,1)}), bf16[4,64,128]{2,1,0:T(8,128)(2,1)S(1)}, u32[]{:S(2)}, u32[]{:S(2)}) %all-to-all-start.2) | async-done | bytes 65568 | tf_op jit(solution)/shard_map/all_to_all | solution.py:73
  174.7 0.1 fusion.14
  174.8 0.7 fusion.16
  175.6 0.0 copy-done.1
  (6 shorter events, 0.0 us)
Async XLA Ops:
  6.5 9.6 %copy-start = (bf16[20,512,128]{2,1,0:T(8,128)(2,1)S(1)}, bf16[20,512,128]{2,1,0:T(8,128)(2,1)}, u32[]{:S(2)}) copy-start(bf16[20,512,128]{2,1,0:T(8,128)(2,1)} %param.16) | copy-start | bytes 7864324
  8.0 70.4 %all-to-all-start.1 = ((s32[8,1,1]{2,1,0:T(1,128)}), s32[8,1,1]{2,1,0:T(1,128)S(1)}, u32[]{:S(2)}, u32[]{:S(2)}) async-start(s32[8,1,1]{2,1,0:T(1,128)} %copy.24), calls=%async_computation.1 | async-start | bytes 8192 | tf_op jit(solution)/shard_map/all_to_all | solution.py:58
  78.4 12.4 %all-to-all-start = ((s32[8,1,32]{2,1,0:T(1,128)}), s32[8,1,32]{2,1,0:T(1,128)S(1)}, u32[]{:S(2)}, u32[]{:S(2)}) async-start(s32[8,1,32]{2,1,0:T(1,128)} %bitcast), calls=%async_computation | async-start | bytes 8192 | tf_op jit(solution)/shard_map/all_to_all | solution.py:57
  84.4 81.2 %reduce-scatter.2.cloned.1.call-start = ((), (), s32[]{:S(2)}) async-start(), calls=%async_computation.4 | async-start | bytes 1179648 | tf_op jit(solution)/shard_map/reduce_scatter | solution.py:68
  90.8 84.8 %copy-start.1 = (bf16[20,512,128]{2,1,0:T(8,128)(2,1)S(1)}, bf16[20,512,128]{2,1,0:T(8,128)(2,1)}, u32[]{:S(2)}) copy-start(bf16[20,512,128]{2,1,0:T(8,128)(2,1)} %param.16) | copy-start | bytes 7864324
  90.8 13.2 %copy-start.5 = (bf16[128]{0:T(256)(128)(2,1)S(1)}, bf16[128]{0:T(256)(128)(2,1)}, u32[]{:S(2)}) copy-start(bf16[128]{0:T(256)(128)(2,1)} %param.18) | copy-start | bytes 772
  90.8 74.8 %copy-start.2 = (bf16[256,512]{1,0:T(8,128)(2,1)S(1)}, bf16[256,512]{1,0:T(8,128)(2,1)}, u32[]{:S(2)}) copy-start(bf16[256,512]{1,0:T(8,128)(2,1)} %param.10) | copy-start | bytes 786436
  90.8 74.8 %copy-start.3 = (bf16[512,128]{1,0:T(8,128)(2,1)S(1)}, bf16[512,128]{1,0:T(8,128)(2,1)}, u32[]{:S(2)}) copy-start(bf16[512,128]{1,0:T(8,128)(2,1)} %param.17) | copy-start | bytes 393220
  90.8 79.8 %copy-start.4 = (bf16[512]{0:T(512)(128)(2,1)S(1)}, bf16[512]{0:T(512)(128)(2,1)}, u32[]{:S(2)}) copy-start(bf16[512]{0:T(512)(128)(2,1)} %param.19) | copy-start | bytes 3076
  167.3 7.4 %all-to-all-start.2 = ((bf16[4,64,128]{2,1,0:T(8,128)(2,1)}), bf16[4,64,128]{2,1,0:T(8,128)(2,1)S(1)}, u32[]{:S(2)}, u32[]{:S(2)}) async-start(bf16[4,64,128]{2,1,0:T(8,128)(2,1)} %bitcast.11), calls=%async_computation.3 | async-start | bytes 131072 | tf_op jit(solution)/shard_map/all_to_all | solution.py:73
Sparse Core Ops, SparseCore 0:
  104.1 61.4 reduce-scatter.1
where the time goes:
time: 184 us; the launch traced here: 182 us
  waiting for transfers between devices  71.8 us (39%)
  local copies, waits for them, and re-layouts  50.8 us (28%)
  matrix products  27.9 us (15%)
  starting transfers between devices  16.6 us (9%)
  between operations  13.5 us (7%)
  other arithmetic  1.89 us (1%)
    reduce_scatter x1, waiting for transfers between devices, per_device(): lax.psum_scatter(summed.reshape(receivers * blocks * BLK, columns), 'dp',...  61.6 us
    reshape x1, local copies, waits for them, and re-layouts, per_device(): transform_slots(lookup, lookup_rows, flat_tiles)  18.2 us
    dot_general x1, local copies, waits for them, and re-layouts, transform_slots(): jnp.einsum('nij,njc->nic', adj_tiles, chosen, preferred_element_type=jnp....  17.4 us
    dot_general x1, matrix products, transform_slots(): jnp.einsum('nij,njc->nic', adj_tiles, chosen, preferred_element_type=jnp....  13.2 us
    dot_general x1, matrix products, per_device(): jnp.einsum('rkb,rkx->rbx', weights, message, precision=lax.Precision.HIGH...  10 us
    gather x1, local copies, waits for them, and re-layouts, transform_slots(): chosen = jnp.take(lookup, lookup_rows, axis=0)  8.62 us
    all_to_all x1, starting transfers between devices, per_device(): lax.all_to_all(live_count.reshape(peer_count, 1), 'dp', split_axis=0, con...  7.28 us
    all_to_all x1, waiting for transfers between devices, per_device(): lax.all_to_all(target_block, 'dp', split_axis=0, concat_axis=0, tiled=True)  6.06 us
  transfers between devices with their start and end apart: 4, of which 3 were waited for; matrix products, arithmetic and copies ran while one was open for 35% of the time, Pallas kernels for 0%

commit v1 on v0

v1 whole, which is shorter than its diff:
```python
import functools

import jax
import jax.numpy as jnp
from jax import lax
from jax.experimental import pallas as pl
from jax.experimental.pallas import tpu as pltpu
from jax.sharding import PartitionSpec as P

BLK = 128
PAIR = 2
LANES = 128
epsilon = 1e-05


def kernel(
    peers,
    groups,
    x_ref,
    sb_ref,
    et_ref,
    tb_ref,
    lc_ref,
    sw_ref,
    bias_ref,
    gain_ref,
    adj_hbm,
    rw_hbm,
    out_ref,
    adj,
    rw,
    table,
    code_out,
    code_in,
    code_sm,
    own,
    pbuf,
    rbuf,
    zbuf,
    zin,
    hid,
    gath,
    rw_sem,
    adj_sem,
    code_send,
    code_recv,
    sm_sem,
    x_send,
    x_recv,
    z_send,
    z_recv,
    h_send,
    h_recv,
):
    me = lax.axis_index("dp")
    col = lax.axis_index("mp")
    outer = peers // PAIR
    zz = me // PAIR
    xx = me % PAIR
    relations = rw_hbm.shape[0]
    slots = adj_hbm.shape[1]
    rows = x_ref.shape[0]
    blocks = rows // BLK
    columns = sw_ref.shape[1]
    zero_tile = blocks * relations
    part = rows // groups

    def dp_peer(offset):
        return lax.rem(me + offset, peers)

    def mp_peer(offset):
        return lax.rem(col + offset, groups)

    barrier = pltpu.get_barrier_semaphore()
    for offset in range(1, peers):
        pl.semaphore_signal(barrier, inc=1, device_id={"dp": dp_peer(offset)})
    for offset in range(1, groups):
        pl.semaphore_signal(barrier, inc=1, device_id={"mp": mp_peer(offset)})

    rw_copies = [
        pltpu.make_async_copy(rw_hbm.at[pl.ds(r, 2)], rw.at[pl.ds(r, 2)], rw_sem.at[r // 2])
        for r in range(0, relations, 2)
    ]
    for copy in rw_copies:
        copy.start()

    def receiver_of(i, side):
        return lax.rem(zz + 1 + i, outer) * PAIR + side

    def adj_copy(d):
        return pltpu.make_async_copy(adj_hbm.at[d], adj.at[d], adj_sem.at[d])

    def start_adj(side):
        def go(i, carry):
            adj_copy(receiver_of(i, side)).start()
            return carry

        lax.fori_loop(0, outer, go, 0)

    start_adj(1 - xx)
    start_adj(xx)

    code_out[...] = jnp.full(code_out.shape, -1, jnp.int32)
    slot_ids = lax.broadcasted_iota(jnp.int32, (1, slots), 1)
    for s in range(peers):
        live = slot_ids < lc_ref[0, s]
        code_out[s, :, 0:slots] = jnp.where(live, tb_ref[s : s + 1, :], -1)
    table[zero_tile] = jnp.zeros((BLK, columns), jnp.bfloat16)

    pl.semaphore_wait(barrier, peers - 1 + groups - 1)

    def code_copy(offset):
        to = dp_peer(offset)
        return pltpu.make_async_remote_copy(
            src_ref=code_out.at[to],
            dst_ref=code_in.at[me],
            send_sem=code_send.at[offset],
            recv_sem=code_recv.at[offset],
            device_id={"dp": to},
        )

    for offset in range(1, peers):
        code_copy(offset).start()
    code_in[me] = code_out[me]

    x = x_ref[...]
    for r in range(0, relations, 2):
        rw_copies[r // 2].wait()
        w = jnp.concatenate([rw[r], rw[r + 1]], axis=1)
        t = jnp.dot(x, w, preferred_element_type=jnp.float32).astype(jnp.bfloat16)
        for b in range(blocks):
            for j in range(2):
                table[b * relations + r + j] = t[
                    b * BLK : (b + 1) * BLK, j * columns : (j + 1) * columns
                ]
    base = jnp.dot(x, sw_ref[...], preferred_element_type=jnp.float32)
    own[...] = base + bias_ref[...].astype(jnp.float32)

    for offset in range(1, peers):
        code_copy(offset).wait()
    to_smem = pltpu.make_async_copy(code_in, code_sm, sm_sem)
    to_smem.start()
    to_smem.wait()

    def sums(d):
        adj_copy(d).wait()
        acc = jnp.zeros((BLK, blocks * columns), jnp.float32)
        step = 2
        for k in range(0, slots, step):
            lhs, rhs = [], []
            for j in range(k, k + step):
                code = code_sm[d, 0, j]
                row = sb_ref[d, j] * relations + et_ref[d, j]
                lhs.append(adj[d, j])
                rhs.append(
                    jnp.concatenate(
                        [table[jnp.where(code == b, row, zero_tile)] for b in range(blocks)],
                        axis=1,
                    )
                )
            acc = acc + jnp.dot(
                jnp.concatenate(lhs, axis=1),
                jnp.concatenate(rhs, axis=0),
                preferred_element_type=jnp.float32,
            )
        return jnp.concatenate(
            [acc[:, b * columns : (b + 1) * columns] for b in range(blocks)], axis=0
        )

    def x_copy(i):
        return pltpu.make_async_remote_copy(
            src_ref=pbuf.at[i],
            dst_ref=rbuf.at[i],
            send_sem=x_send.at[i],
            recv_sem=x_recv.at[i],
            device_id={"dp": zz * PAIR + 1 - xx},
        )

    def z_copy(i):
        return pltpu.make_async_remote_copy(
            src_ref=zbuf.at[i],
            dst_ref=zin.at[i],
            send_sem=z_send.at[i],
            recv_sem=z_recv.at[i],
            device_id={"dp": receiver_of(i, xx)},
        )

    def partner_step(i, carry):
        pbuf[i] = sums(receiver_of(i, 1 - xx)).astype(jnp.bfloat16)
        x_copy(i).start()
        return carry

    lax.fori_loop(0, outer, partner_step, 0)

    def own_step(i, carry):
        mine = sums(receiver_of(i, xx))
        x_copy(i).wait()
        zbuf[i] = (mine + rbuf[i].astype(jnp.float32)).astype(jnp.bfloat16)
        z_copy(i).start()
        return carry

    lax.fori_loop(0, outer - 1, own_step, 0)

    own[...] += sums(me)
    x_copy(outer - 1).wait()
    own[...] += rbuf[outer - 1].astype(jnp.float32)

    def arrive(i, carry):
        z_copy(i).wait()
        own[...] += zin[i].astype(jnp.float32)
        return carry

    lax.fori_loop(0, outer - 1, arrive, 0)

    hid[...] = jnp.maximum(own[...], 0.0).astype(jnp.bfloat16)

    def h_copy(offset):
        to = mp_peer(offset)
        return pltpu.make_async_remote_copy(
            src_ref=hid.at[pl.ds(pl.multiple_of(to * part, part), part)],
            dst_ref=gath.at[col],
            send_sem=h_send.at[offset],
            recv_sem=h_recv.at[offset],
            device_id={"mp": to},
        )

    for offset in range(1, groups):
        h_copy(offset).start()
    gath[col] = hid[pl.ds(pl.multiple_of(col * part, part), part)]
    for offset in range(1, groups):
        h_copy(offset).wait()
    values = jnp.concatenate([gath[g] for g in range(groups)], axis=1).astype(jnp.float32)
    inverse_rms = lax.rsqrt(jnp.mean(values * values, axis=1, keepdims=True) + epsilon)
    out_ref[...] = (values * inverse_rms * gain_ref[...].astype(jnp.float32)).astype(jnp.bfloat16)


def per_device(
    features,
    adjacency,
    source_block,
    edge_type,
    target_block,
    live_count,
    relation_weight,
    self_weight,
    layer_bias,
    norm_gain,
):
    peers = lax.axis_size("dp")
    groups = lax.axis_size("mp")
    rows, width = features.shape
    relations, _, columns = relation_weight.shape
    blocks = rows // BLK
    outer = peers // PAIR
    part = rows // groups
    vmem = pl.BlockSpec(memory_space=pltpu.VMEM)
    smem = pl.BlockSpec(memory_space=pltpu.SMEM)
    hbm = pl.BlockSpec(memory_space=pl.ANY)
    dma = pltpu.SemaphoreType.DMA
    return pl.pallas_call(
        functools.partial(kernel, peers, groups),
        out_shape=jax.ShapeDtypeStruct((part, width), jnp.bfloat16),
        in_specs=[vmem, smem, smem, vmem, smem, vmem, vmem, vmem, hbm, hbm],
        out_specs=vmem,
        scratch_shapes=[
            pltpu.VMEM(adjacency.shape, jnp.bfloat16),
            pltpu.VMEM(relation_weight.shape, jnp.bfloat16),
            pltpu.VMEM((blocks * relations + 1, BLK, columns), jnp.bfloat16),
            pltpu.VMEM((peers, 1, LANES), jnp.int32),
            pltpu.VMEM((peers, 1, LANES), jnp.int32),
            pltpu.SMEM((peers, 1, LANES), jnp.int32),
            pltpu.VMEM((rows, columns), jnp.float32),
            pltpu.VMEM((outer, rows, columns), jnp.bfloat16),
            pltpu.VMEM((outer, rows, columns), jnp.bfloat16),
            pltpu.VMEM((outer, rows, columns), jnp.bfloat16),
            pltpu.VMEM((outer, rows, columns), jnp.bfloat16),
            pltpu.VMEM((rows, columns), jnp.bfloat16),
            pltpu.VMEM((groups, part, columns), jnp.bfloat16),
            dma((relations // 2,)),
            dma((peers,)),
            dma((peers,)),
            dma((peers,)),
            dma,
            dma((outer,)),
            dma((outer,)),
            dma((outer,)),
            dma((outer,)),
            dma((groups,)),
            dma((groups,)),
        ],
        compiler_params=pltpu.CompilerParams(collective_id=0, has_side_effects=True),
    )(
        features,
        source_block,
        edge_type,
        target_block,
        live_count,
        self_weight,
        layer_bias.reshape(1, columns),
        norm_gain.reshape(1, width),
        adjacency,
        relation_weight,
    )


def solution(mesh):
    return jax.shard_map(
        per_device,
        mesh=mesh,
        in_specs=(
            P("dp", None),
            P("dp", None, None, None),
            P("dp", None),
            P("dp", None),
            P("dp", None),
            P("dp", None),
            P(None, None, "mp"),
            P(None, "mp"),
            P("mp"),
            P(),
        ),
        out_specs=P(("dp", "mp"), None),
        check_vma=False,
    )
```

time: 184 us -> 28.9 us (0.16)
  waiting for transfers between devices: 71.8 us -> 0 us
  local copies, waits for them, and re-layouts: 50.8 us -> 2.73 us
  matrix products: 27.9 us -> 0 us
  Pallas kernels: 0 us -> 26 us
  starting transfers between devices: 16.6 us -> 0 us
  between operations: 13.5 us -> 0.01 us
  other arithmetic: 1.89 us -> 0 us
    reduce_scatter x1 -> x0, waiting for transfers between devices: 61.6 us -> none  [per_device(): lax.psum_scatter(summed.reshape(receivers * blocks * BLK, columns), 'dp',...]
    dot_general x4 -> x0, matrix products: 27.9 us -> none  [the longest x1 13.2 us: transform_slots(): jnp.einsum('nij,njc->nic', adj_tiles, chosen, preferred_element_type=jnp....]
    pallas_call x0 -> x1, Pallas kernels: none -> 26 us  [per_device(): pl.pallas_call(functools.partial(kernel, peers, groups), out_shape=jax.Sh...]
    reshape x4 -> x1, local copies, waits for them, and re-layouts: 21.5 us -> 1.26 us  [per_device(): norm_gain.reshape(1, width)]
    dot_general x1 -> x0, local copies, waits for them, and re-layouts: 17.4 us -> none  [transform_slots(): jnp.einsum('nij,njc->nic', adj_tiles, chosen, preferred_element_type=jnp....]
    all_to_all x3 -> x0, starting transfers between devices: 16.6 us -> none  [the longest x1 7.28 us: per_device(): lax.all_to_all(live_count.reshape(peer_count, 1), 'dp', split_axis=0, con...]
    all_to_all x3 -> x0, waiting for transfers between devices: 10.1 us -> none  [the longest x1 6.06 us: per_device(): lax.all_to_all(target_block, 'dp', split_axis=0, concat_axis=0, tiled=True)]
    gather x1 -> x0, local copies, waits for them, and re-layouts: 8.62 us -> none  [transform_slots(): chosen = jnp.take(lookup, lookup_rows, axis=0)]
  transfers between devices with their start and end apart: 4 -> 0, of which waited for: 3 -> 0; matrix products, arithmetic and copies ran while one was open for 35% -> 0% of each run, Pallas kernels for 0% -> 0%
where the time goes in v1:
time: 28.9 us; the launch traced here: 28.7 us
  Pallas kernels  26 us (90%)
  local copies, waits for them, and re-layouts  2.73 us (9%)
    pallas_call x1, Pallas kernels, per_device(): pl.pallas_call(functools.partial(kernel, peers, groups), out_shape=jax.Sh...  26 us
    unnamed x1, local copies, waits for them, and re-layouts  1.47 us
    reshape x1, local copies, waits for them, and re-layouts, per_device(): norm_gain.reshape(1, width)  1.26 us

profile of v1, /device:TPU:0, one launch (start us, length us, event | category | flops | bytes accessed | tf_op | source)
XLA Modules:
  0.0 28.7 jit_solution(10448513903495127911)
XLA Ops:
  0.0 1.3 %reshape.7.gain_ref = bf16[1,512]{1,0:T(2,128)(2,1)} reshape(bf16[512]{0:T(512)(128)(2,1)} %param.19) | data formatting | bytes 2048 | tf_op jit(solution)/shard_map/reshape | solution.py:300
  1.3 26.0 %shard_map.100 = bf16[64,512]{1,0:T(8,128)(2,1)} custom-call(bf16[256,512]{1,0:T(8,128)(2,1)} %x_ref.1, s32[8,32]{1,0:T(8,128)} %sb_ref.1, s32[8,32]{1,0:T(8,128)} %et_ref.1, s32[8,32]{1,0:T(8,128)} %tb_ref.1, s32[1,8]{1,0:T(1,128)} %lc_ref.1, bf16[512,128]{1,0:T(8,128)(2,1)} %sw_ref.1, bf16[1,128]{1,0:T(2,128)(2,1)} %bitcast.1, ...), custom_call_target="tpu_custom_call" | custom-call | tf_op jit(solution)/shard_map/pallas_call | solution.py:260
  27.3 1.5 %copy.12 = bf16[64,512]{1,0:T(8,128)(2,1)} copy(bf16[64,512]{1,0:T(8,128)(2,1)} %shard_map.100) | data formatting | bytes 131072

commit v2 on v1

v2 whole, which is shorter than its diff:
```python
import functools

import jax
import jax.numpy as jnp
from jax import lax
from jax.experimental import pallas as pl
from jax.experimental.pallas import tpu as pltpu
from jax.sharding import PartitionSpec as P

BLK = 128
PAIR = 2
LANES = 128
epsilon = 1e-05


def kernel(
    peers,
    groups,
    x_hbm,
    sb_hbm,
    et_hbm,
    tb_hbm,
    lc_hbm,
    sw_hbm,
    bias_hbm,
    gain_hbm,
    adj_hbm,
    rw_hbm,
    out_ref,
    x_ref,
    sb_ref,
    et_ref,
    tb_ref,
    lc_ref,
    sw_ref,
    bias_ref,
    gain_ref,
    adj,
    rw,
    table,
    code_out,
    code_in,
    code_sm,
    own,
    pbuf,
    rbuf,
    zbuf,
    zin,
    in_sem,
    rw_sem,
    adj_sem,
    code_send,
    code_recv,
    sm_sem,
    x_send,
    x_recv,
    z_send,
    z_recv,
):
    me = lax.axis_index("dp")
    col = lax.axis_index("mp")
    outer = peers // PAIR
    zz = me // PAIR
    xx = me % PAIR
    relations = rw_hbm.shape[0]
    slots = adj_hbm.shape[1]
    rows = x_hbm.shape[0]
    blocks = rows // BLK
    columns = sw_hbm.shape[1]
    zero_tile = blocks * relations
    part = rows // groups

    def dp_peer(offset):
        return lax.rem(me + offset, peers)

    def mp_peer(offset):
        return lax.rem(col + offset, groups)

    def z_peer(offset):
        return lax.rem(zz + offset, outer)

    barrier = pltpu.get_barrier_semaphore()
    for zo in range(outer):
        pl.semaphore_signal(barrier, inc=1, device_id={"dp": z_peer(zo) * PAIR + 1 - xx})
        for mo in range(groups):
            if zo or mo:
                pl.semaphore_signal(
                    barrier, inc=1, device_id={"dp": z_peer(zo) * PAIR + xx, "mp": mp_peer(mo)}
                )

    pairs = (
        (tb_hbm, tb_ref),
        (lc_hbm, lc_ref),
        (x_hbm, x_ref),
        (sb_hbm, sb_ref),
        (et_hbm, et_ref),
        (sw_hbm, sw_ref),
        (bias_hbm, bias_ref),
        (gain_hbm, gain_ref),
    )
    in_copies = [
        pltpu.make_async_copy(src, dst, in_sem.at[n]) for n, (src, dst) in enumerate(pairs)
    ]
    for copy in in_copies[:3]:
        copy.start()

    rw_copies = [
        pltpu.make_async_copy(rw_hbm.at[pl.ds(r, 2)], rw.at[pl.ds(r, 2)], rw_sem.at[r // 2])
        for r in range(0, relations, 2)
    ]
    for copy in rw_copies:
        copy.start()
    for copy in in_copies[3:]:
        copy.start()

    def receiver_of(i, side):
        down = outer - 1 - i
        down = jnp.where(down <= zz, down - 1, down)
        up = jnp.where(i < zz, i, i + 1)
        to = jnp.where(zz < outer // 2, down, up)
        return jnp.where(i == outer - 1, zz, to) * PAIR + side

    def adj_copy(d):
        return pltpu.make_async_copy(adj_hbm.at[d], adj.at[d], adj_sem.at[d])

    def start_adj(side):
        def go(i, carry):
            adj_copy(receiver_of(i, side)).start()
            return carry

        lax.fori_loop(0, outer, go, 0)

    start_adj(1 - xx)
    start_adj(xx)

    in_copies[0].wait()
    in_copies[1].wait()
    code_out[...] = jnp.full(code_out.shape, -1, jnp.int32)
    slot_ids = lax.broadcasted_iota(jnp.int32, (1, slots), 1)
    for s in range(peers):
        live = slot_ids < lc_ref[0, s]
        code_out[s, :, 0:slots] = jnp.where(live, tb_ref[s : s + 1, :], -1)
    table[zero_tile] = jnp.zeros((BLK, columns), jnp.bfloat16)

    in_copies[2].wait()
    x = x_ref[...]
    for r in range(0, relations, 2):
        rw_copies[r // 2].wait()
        w = jnp.concatenate([rw[r], rw[r + 1]], axis=1)
        t = jnp.dot(x, w, preferred_element_type=jnp.float32).astype(jnp.bfloat16)
        for b in range(blocks):
            for j in range(2):
                table[b * relations + r + j] = t[
                    b * BLK : (b + 1) * BLK, j * columns : (j + 1) * columns
                ]

    pl.semaphore_wait(barrier, outer * groups - 1 + outer)

    def code_copy(offset):
        to = dp_peer(offset)
        return pltpu.make_async_remote_copy(
            src_ref=code_out.at[to],
            dst_ref=code_in.at[me],
            send_sem=code_send.at[offset],
            recv_sem=code_recv.at[offset],
            device_id={"dp": to},
        )

    for offset in range(1, peers):
        code_copy(offset).start()
    code_in[me] = code_out[me]

    for copy in in_copies[3:]:
        copy.wait()
    base = jnp.dot(x, sw_ref[...], preferred_element_type=jnp.float32)
    own[...] = base + bias_ref[...].astype(jnp.float32)

    for offset in range(1, peers):
        code_copy(offset).wait()
    to_smem = pltpu.make_async_copy(code_in, code_sm, sm_sem)
    to_smem.start()
    to_smem.wait()

    def sums(d):
        adj_copy(d).wait()
        acc = jnp.zeros((BLK, blocks * columns), jnp.float32)
        step = 2
        for k in range(0, slots, step):
            lhs, rhs = [], []
            for j in range(k, k + step):
                code = code_sm[d, 0, j]
                row = sb_ref[d, j] * relations + et_ref[d, j]
                lhs.append(adj[d, j])
                rhs.append(
                    jnp.concatenate(
                        [table[jnp.where(code == b, row, zero_tile)] for b in range(blocks)],
                        axis=1,
                    )
                )
            acc = acc + jnp.dot(
                jnp.concatenate(lhs, axis=1),
                jnp.concatenate(rhs, axis=0),
                preferred_element_type=jnp.float32,
            )
        return jnp.concatenate(
            [acc[:, b * columns : (b + 1) * columns] for b in range(blocks)], axis=0
        )

    def x_copy(i):
        return pltpu.make_async_remote_copy(
            src_ref=pbuf.at[i],
            dst_ref=rbuf.at[i],
            send_sem=x_send.at[i],
            recv_sem=x_recv.at[i],
            device_id={"dp": zz * PAIR + 1 - xx},
        )

    def z_copy(i, to, group, src):
        return pltpu.make_async_remote_copy(
            src_ref=zbuf.at[i, pl.ds(pl.multiple_of(group * part, part), part)],
            dst_ref=zin.at[src],
            send_sem=z_send.at[i, group],
            recv_sem=z_recv.at[src],
            device_id={"dp": to, "mp": group},
        )

    mine = zz * groups + col

    def partner_step(i, carry):
        pbuf[i] = sums(receiver_of(i, 1 - xx)).astype(jnp.bfloat16)
        x_copy(i).start()
        return carry

    lax.fori_loop(0, outer, partner_step, 0)

    def own_step(i, carry):
        held = sums(receiver_of(i, xx))
        x_copy(i).wait_recv()
        zbuf[i] = (held + rbuf[i].astype(jnp.float32)).astype(jnp.bfloat16)
        for mo in range(groups):
            z_copy(i, receiver_of(i, xx), mp_peer(mo), mine).start()
        return carry

    lax.fori_loop(0, outer - 1, own_step, 0)

    last = outer - 1
    held = own[...] + sums(me)
    x_copy(last).wait_recv()
    zbuf[last] = (held + rbuf[last].astype(jnp.float32)).astype(jnp.bfloat16)
    for mo in range(1, groups):
        z_copy(last, me, mp_peer(mo), mine).start()
    zin[mine] = zbuf[last, pl.ds(pl.multiple_of(col * part, part), part)]

    for i in range(outer):
        x_copy(i).wait_send()
        for mo in range(0 if i < last else 1, groups):
            z_copy(i, receiver_of(i, xx), mp_peer(mo), mine).wait_send()
    total = outer * groups
    for n in range(1, total):
        z_copy(0, me, mp_peer(1), lax.rem(mine + n, total)).wait_recv()
    pieces = []
    for g in range(groups):
        piece = zin[g].astype(jnp.float32)
        for z in range(1, outer):
            piece = piece + zin[z * groups + g].astype(jnp.float32)
        pieces.append(jnp.maximum(piece, 0.0).astype(jnp.bfloat16).astype(jnp.float32))
    values = jnp.concatenate(pieces, axis=1)
    gain = jnp.concatenate([gain_ref[n : n + 1, :] for n in range(gain_ref.shape[0])], axis=1)
    inverse_rms = lax.rsqrt(jnp.mean(values * values, axis=1, keepdims=True) + epsilon)
    out_ref[...] = (values * inverse_rms * gain.astype(jnp.float32)).astype(jnp.bfloat16)


def per_device(
    features,
    adjacency,
    source_block,
    edge_type,
    target_block,
    live_count,
    relation_weight,
    self_weight,
    layer_bias,
    norm_gain,
):
    peers = lax.axis_size("dp")
    groups = lax.axis_size("mp")
    rows, width = features.shape
    relations, _, columns = relation_weight.shape
    blocks = rows // BLK
    outer = peers // PAIR
    part = rows // groups
    vmem = pl.BlockSpec(memory_space=pltpu.VMEM)
    hbm = pl.BlockSpec(memory_space=pl.ANY)
    dma = pltpu.SemaphoreType.DMA
    return pl.pallas_call(
        functools.partial(kernel, peers, groups),
        out_shape=jax.ShapeDtypeStruct((part, width), jnp.bfloat16),
        in_specs=[hbm] * 10,
        out_specs=vmem,
        scratch_shapes=[
            pltpu.VMEM(features.shape, jnp.bfloat16),
            pltpu.SMEM(source_block.shape, jnp.int32),
            pltpu.SMEM(edge_type.shape, jnp.int32),
            pltpu.VMEM(target_block.shape, jnp.int32),
            pltpu.SMEM(live_count.shape, jnp.int32),
            pltpu.VMEM(self_weight.shape, jnp.bfloat16),
            pltpu.VMEM((1, columns), jnp.bfloat16),
            pltpu.VMEM((width // LANES, LANES), jnp.bfloat16),
            pltpu.VMEM(adjacency.shape, jnp.bfloat16),
            pltpu.VMEM(relation_weight.shape, jnp.bfloat16),
            pltpu.VMEM((blocks * relations + 1, BLK, columns), jnp.bfloat16),
            pltpu.VMEM((peers, 1, LANES), jnp.int32),
            pltpu.VMEM((peers, 1, LANES), jnp.int32),
            pltpu.SMEM((peers, 1, LANES), jnp.int32),
            pltpu.VMEM((rows, columns), jnp.float32),
            pltpu.VMEM((outer, rows, columns), jnp.bfloat16),
            pltpu.VMEM((outer, rows, columns), jnp.bfloat16),
            pltpu.VMEM((outer, rows, columns), jnp.bfloat16),
            pltpu.VMEM((outer * groups, part, columns), jnp.bfloat16),
            dma((8,)),
            dma((relations // 2,)),
            dma((peers,)),
            dma((peers,)),
            dma((peers,)),
            dma,
            dma((outer,)),
            dma((outer,)),
            dma((outer, groups)),
            dma((outer * groups,)),
        ],
        compiler_params=pltpu.CompilerParams(collective_id=0, has_side_effects=True),
    )(
        features,
        source_block,
        edge_type,
        target_block,
        live_count,
        self_weight,
        layer_bias.reshape(1, columns),
        norm_gain.reshape(width // LANES, LANES),
        adjacency,
        relation_weight,
    )


def solution(mesh):
    return jax.shard_map(
        per_device,
        mesh=mesh,
        in_specs=(
            P("dp", None),
            P("dp", None, None, None),
            P("dp", None),
            P("dp", None),
            P("dp", None),
            P("dp", None),
            P(None, None, "mp"),
            P(None, "mp"),
            P("mp"),
            P(),
        ),
        out_specs=P(("dp", "mp"), None),
        check_vma=False,
    )
```

time: 28.9 us -> 25.6 us (0.89)
  Pallas kernels: 26 us -> 23.9 us
  local copies, waits for them, and re-layouts: 2.73 us -> 1.47 us
    pallas_call x1, Pallas kernels: 26 us -> 23.9 us  [per_device(): pl.pallas_call(functools.partial(kernel, peers, groups), out_shape=jax.Sh...]
    reshape x1 -> x0, local copies, waits for them, and re-layouts: 1.26 us -> none  [per_device(): norm_gain.reshape(1, width)]
where the time goes in v2:
time: 25.6 us; the launch traced here: 25.4 us
  Pallas kernels  23.9 us (93%)
  local copies, waits for them, and re-layouts  1.47 us (6%)
    pallas_call x1, Pallas kernels, per_device(): pl.pallas_call(functools.partial(kernel, peers, groups), out_shape=jax.Sh...  23.9 us
    unnamed x1, local copies, waits for them, and re-layouts  1.47 us

profile of v2, /device:TPU:0, one launch (start us, length us, event | category | flops | bytes accessed | tf_op | source)
XLA Modules:
  0.0 25.4 jit_solution(12162596029163399401)
XLA Ops:
  0.0 23.9 %shard_map.100 = bf16[64,512]{1,0:T(8,128)(2,1)} custom-call(bf16[256,512]{1,0:T(8,128)(2,1)} %x_hbm.1, s32[8,32]{1,0:T(8,128)} %sb_hbm.1, s32[8,32]{1,0:T(8,128)} %et_hbm.1, s32[8,32]{1,0:T(8,128)} %tb_hbm.1, s32[1,8]{1,0:T(1,128)} %lc_hbm.1, bf16[512,128]{1,0:T(8,128)(2,1)} %sw_hbm.1, bf16[1,128]{1,0:T(2,128)(2,1)} %bitcast.3, bf16[4,128]{1,0:T(4,128)(2,1)} %bitcast.2, ...), custom_call_target="tpu_custom_call" | custom-call | tf_op jit(solution)/shard_map/pallas_call | solution.py:295
  23.9 1.5 %copy.12 = bf16[64,512]{1,0:T(8,128)(2,1)} copy(bf16[64,512]{1,0:T(8,128)(2,1)} %shard_map.100) | data formatting | bytes 131072

commit v3 on v2

--- a/solution.py
+++ b/solution.py
@@ -113,19 +113,20 @@
     for copy in in_copies[3:]:
         copy.start()
 
-    def receiver_of(i, side):
+    def near_first(step):
+        i = outer - 1 - step
         down = outer - 1 - i
         down = jnp.where(down <= zz, down - 1, down)
         up = jnp.where(i < zz, i, i + 1)
         to = jnp.where(zz < outer // 2, down, up)
-        return jnp.where(i == outer - 1, zz, to) * PAIR + side
+        return jnp.where(i == outer - 1, zz, to)
 
     def adj_copy(d):
         return pltpu.make_async_copy(adj_hbm.at[d], adj.at[d], adj_sem.at[d])
 
     def start_adj(side):
         def go(i, carry):
-            adj_copy(receiver_of(i, side)).start()
+            adj_copy(near_first(i) * PAIR + side).start()
             return carry
 
         lax.fori_loop(0, outer, go, 0)
@@ -175,13 +176,20 @@
     base = jnp.dot(x, sw_ref[...], preferred_element_type=jnp.float32)
     own[...] = base + bias_ref[...].astype(jnp.float32)
 
-    for offset in range(1, peers):
-        code_copy(offset).wait()
-    to_smem = pltpu.make_async_copy(code_in, code_sm, sm_sem)
-    to_smem.start()
-    to_smem.wait()
+    def await_code(d):
+        offset = lax.rem(me - d + peers, peers)
+        pltpu.make_async_remote_copy(
+            src_ref=code_out.at[d],
+            dst_ref=code_in.at[d],
+            send_sem=code_send.at[offset],
+            recv_sem=code_recv.at[offset],
+            device_id={"dp": d},
+        ).wait_recv()
 
     def sums(d):
+        to_smem = pltpu.make_async_copy(code_in.at[d], code_sm.at[d], sm_sem)
+        to_smem.start()
+        to_smem.wait()
         adj_copy(d).wait()
         acc = jnp.zeros((BLK, blocks * columns), jnp.float32)
         step = 2
@@ -226,35 +234,43 @@
 
     mine = zz * groups + col
 
-    def partner_step(i, carry):
-        pbuf[i] = sums(receiver_of(i, 1 - xx)).astype(jnp.bfloat16)
-        x_copy(i).start()
+    def partner_step(step, carry):
+        z = near_first(step)
+        d = z * PAIR + 1 - xx
+        await_code(d)
+        pbuf[z] = sums(d).astype(jnp.bfloat16)
+        x_copy(z).start()
         return carry
 
     lax.fori_loop(0, outer, partner_step, 0)
 
-    def own_step(i, carry):
-        held = sums(receiver_of(i, xx))
-        x_copy(i).wait_recv()
-        zbuf[i] = (held + rbuf[i].astype(jnp.float32)).astype(jnp.bfloat16)
+    def own_step(step, carry):
+        z = near_first(step)
+        d = z * PAIR + xx
+        await_code(d)
+        held = sums(d)
+        x_copy(z).wait_recv()
+        zbuf[z] = (held + rbuf[z].astype(jnp.float32)).astype(jnp.bfloat16)
         for mo in range(groups):
-            z_copy(i, receiver_of(i, xx), mp_peer(mo), mine).start()
+            z_copy(z, d, mp_peer(mo), mine).start()
         return carry
 
-    lax.fori_loop(0, outer - 1, own_step, 0)
-
-    last = outer - 1
+    lax.fori_loop(1, outer, own_step, 0)
+
     held = own[...] + sums(me)
-    x_copy(last).wait_recv()
-    zbuf[last] = (held + rbuf[last].astype(jnp.float32)).astype(jnp.bfloat16)
+    x_copy(zz).wait_recv()
+    zbuf[zz] = (held + rbuf[zz].astype(jnp.float32)).astype(jnp.bfloat16)
     for mo in range(1, groups):
-        z_copy(last, me, mp_peer(mo), mine).start()
-    zin[mine] = zbuf[last, pl.ds(pl.multiple_of(col * part, part), part)]
-
-    for i in range(outer):
-        x_copy(i).wait_send()
-        for mo in range(0 if i < last else 1, groups):
-            z_copy(i, receiver_of(i, xx), mp_peer(mo), mine).wait_send()
+        z_copy(zz, me, mp_peer(mo), mine).start()
+    zin[mine] = zbuf[zz, pl.ds(pl.multiple_of(col * part, part), part)]
+
+    for offset in range(1, peers):
+        code_copy(offset).wait_send()
+    for zo in range(outer):
+        z = z_peer(zo)
+        x_copy(z).wait_send()
+        for mo in range(1 if zo == 0 else 0, groups):
+            z_copy(z, z * PAIR + xx, mp_peer(mo), mine).wait_send()
     total = outer * groups
     for n in range(1, total):
         z_copy(0, me, mp_peer(1), lax.rem(mine + n, total)).wait_recv()

time: 25.6 us -> 27.1 us (1.059)
  Pallas kernels: 23.9 us -> 25.5 us
    pallas_call x1, Pallas kernels: 23.9 us -> 25.5 us  [per_device(): pl.pallas_call(functools.partial(kernel, peers, groups), out_shape=jax.Sh...]
where the time goes in v3:
time: 27.1 us; the launch traced here: 26.9 us
  Pallas kernels  25.5 us (94%)
  local copies, waits for them, and re-layouts  1.47 us (5%)
    pallas_call x1, Pallas kernels, per_device(): pl.pallas_call(functools.partial(kernel, peers, groups), out_shape=jax.Sh...  25.5 us
    unnamed x1, local copies, waits for them, and re-layouts  1.47 us

profile of v3, /device:TPU:0, one launch (start us, length us, event | category | flops | bytes accessed | tf_op | source)
XLA Modules:
  0.0 26.9 jit_solution(16044489073846578962)
XLA Ops:
  0.0 25.5 %shard_map.100 = bf16[64,512]{1,0:T(8,128)(2,1)} custom-call(bf16[256,512]{1,0:T(8,128)(2,1)} %x_hbm.1, s32[8,32]{1,0:T(8,128)} %sb_hbm.1, s32[8,32]{1,0:T(8,128)} %et_hbm.1, s32[8,32]{1,0:T(8,128)} %tb_hbm.1, s32[1,8]{1,0:T(1,128)} %lc_hbm.1, bf16[512,128]{1,0:T(8,128)(2,1)} %sw_hbm.1, bf16[1,128]{1,0:T(2,128)(2,1)} %bitcast.3, bf16[4,128]{1,0:T(4,128)(2,1)} %bitcast.2, ...), custom_call_target="tpu_custom_call" | custom-call | tf_op jit(solution)/shard_map/pallas_call | solution.py:311
  25.5 1.5 %copy.12 = bf16[64,512]{1,0:T(8,128)(2,1)} copy(bf16[64,512]{1,0:T(8,128)(2,1)} %shard_map.100) | data formatting | bytes 131072
